TPU v7x, 32 devices: a whole 2x2x4 slice. The times are simulated.
32 devices in a mesh: rep: 2 (over y), tp: 4 (over z), ep: 4 (over x, core).
Axes of the slice: x: 2, y: 2, z: 4, core: 2. Of those that a mesh axis runs over, the one named last changes fastest.
Arguments:
- tokens: bfloat16 [768, 3072], P(('rep', 'ep'), 'tp'), parts along dimension 0, may hold values from -6 to 6
- routing: int32 [768, 2], P(('rep', 'ep')), parts along dimension 0, may hold values from 0 to 3, all different within a row; in each aligned block of 96 rows (0 to 95, 96 to 191, ...) at most 54 rows name the same one
- route_gates: float32 [768, 2], P(('rep', 'ep')), parts along dimension 0, may hold values from 0.2 to 1
- expert_gate: bfloat16 [4, 3072, 8192], P('ep', None, 'tp'), may hold values from -0.109375 to 0.109375
- expert_up: bfloat16 [4, 3072, 8192], P('ep', None, 'tp'), may hold values from -0.109375 to 0.109375
- expert_down: bfloat16 [4, 8192, 3072], P('ep', 'tp'), may hold values from -0.0625 to 0.0625
Outputs:
- mixture: bfloat16 [768, 3072], P(('rep', 'ep'), 'tp'), parts along dimension 0
There are 2 independent parts, one for each index of `rep`. A program takes and returns all parts, laid end to end along the dimension named above; an argument that names none is the same for every part. Nothing has to cross between parts.
Inputs may be any that keep to these rules, and one draw needn't show every extreme that they name: `routing`: each token names two different experts. In each aligned block of 96 tokens (the rows of one index of ep) no expert is named by more than 54 tokens, a bound that some block reaches.
All inputs are finite; a program needn't handle non-finite values.
Results may differ from a plain program's by a relative error of at most 0.0085.
Values may be sent and summed in bfloat16 or wider, within the bound.
A program may use at most 128 MiB of HBM per device.

v0:
```python
import jax
import jax.numpy as jnp
from jax import lax
from jax.sharding import PartitionSpec as P


def slot_tables(routing, route_gates, experts, capacity):
    count_rows = routing.shape[0]
    choices_n = routing.shape[1]
    flat_ids = routing.reshape(-1)
    onehot = (flat_ids[:, None] == jnp.arange(experts, dtype=jnp.int32)[None, :]).astype(jnp.int32)
    before = jnp.cumsum(onehot, axis=0) - onehot
    position = jnp.sum(before * onehot, axis=1)
    slot_index = flat_ids * capacity + position
    picked = (
        slot_index[:, None] == jnp.arange(experts * capacity, dtype=jnp.int32)[None, :]
    ).astype(jnp.float32)
    dispatch = picked.reshape(count_rows, choices_n, experts * capacity).sum(axis=1)
    combine = (
        (picked * route_gates.reshape(-1)[:, None])
        .reshape(count_rows, choices_n, experts * capacity)
        .sum(axis=1)
    )
    return (dispatch, combine)


def hidden_rows(everyone, expert_gate, expert_up, capacity):
    local_count = expert_gate.shape[0]
    total = everyone.shape[0]
    row_block = everyone.reshape(
        total // (local_count * capacity), local_count, capacity, everyone.shape[1]
    )
    gate_part = jnp.einsum(
        "tlcd,ldf->tlcf", row_block, expert_gate, preferred_element_type=jnp.float32
    )
    upward = jnp.einsum("tlcd,ldf->tlcf", row_block, expert_up, preferred_element_type=jnp.float32)
    return (jax.nn.silu(gate_part) * upward).astype(jnp.bfloat16)


def body(tokens, routing, route_gates, expert_gate, expert_up, expert_down):
    local_count = expert_gate.shape[0]
    ep_count = lax.axis_size("ep")
    tp_count = lax.axis_size("tp")
    tok_count = tokens.shape[0]
    capacity = 2 * tok_count // ep_count + tok_count // 16
    experts = local_count * ep_count
    dispatch, combine = slot_tables(routing, route_gates, experts, capacity)
    dispatch_low = dispatch.astype(jnp.bfloat16)
    whole = lax.all_gather(tokens, "tp", axis=1, tiled=True)
    packed = jnp.einsum(
        "tc,td->cd", dispatch_low, whole, preferred_element_type=jnp.float32
    ).astype(jnp.bfloat16)
    everyone = lax.all_to_all(packed, "ep", split_axis=0, concat_axis=0, tiled=True)
    total_rows = everyone.shape[0]
    columns = everyone.shape[1]
    hidden = hidden_rows(everyone, expert_gate, expert_up, capacity)
    part = jnp.einsum("tlcf,lfd->dtlc", hidden, expert_down, preferred_element_type=jnp.float32)
    summed_t = lax.psum_scatter(
        part.reshape(columns // tp_count * lax.axis_size("tp"), total_rows),
        "tp",
        scatter_dimension=0,
        tiled=True,
    )
    summed = summed_t.T
    expert_out = summed.astype(jnp.bfloat16)
    returned = lax.all_to_all(expert_out, "ep", split_axis=0, concat_axis=0, tiled=True)
    mixed = jnp.dot(combine, returned.astype(jnp.float32), precision=lax.Precision.HIGHEST)
    return mixed.astype(jnp.bfloat16)


def solution(mesh):
    return jax.shard_map(
        body,
        mesh=mesh,
        in_specs=(
            P(("rep", "ep"), "tp"),
            P(("rep", "ep"), None),
            P(("rep", "ep"), None),
            P("ep", None, "tp"),
            P("ep", None, "tp"),
            P("ep", "tp", None),
        ),
        out_specs=P(("rep", "ep"), "tp"),
        check_vma=False,
    )
```

profile of v0, /device:TPU:0, one launch (start us, length us, event | category | flops | bytes accessed | tf_op | source)
XLA Modules:
  0.0 145.9 jit_solution(12279673939200975978)
XLA Ops:
  6.5 0.8 copy.23
  7.3 0.1 eq.37
  7.5 1.2 reduce-window.6
  8.7 0.1 slice.12
  8.8 0.1 copy.24
  8.9 0.1 copy.25
  9.0 0.1 add_bitcast_fusion
  9.1 0.1 reduce_sum.30
  9.3 0.7 multiply_add_fusion
  10.1 18.5 %all_gather.3 = bf16[96,3072]{1,0:T(8,128)(2,1)S(1)} all-gather(bf16[96,768]{1,0:T(8,128)(2,1)} %param.6), channel_id=1, replica_groups=mesh['rep'=2,'tp'=4,'ep'=4] {'tp'}, dimensions={1}, use_global_device_ids=true | all-gather | bytes 737280 | tf_op jit(solution)/shard_map/all_gather | solution.py:49
  28.5 0.8 convert_reduce_fusion
  29.3 0.5 convolution_convert_fusion
  29.9 0.4 all_to_all.14
  30.2 20.5 %all_to_all.21 = bf16[4,54,3072]{2,1,0:T(8,128)(2,1)S(1)} all-to-all(bf16[4,54,3072]{2,1,0:T(8,128)(2,1)S(1)} %all_to_all.14), channel_id=1, replica_groups=mesh['rep'=2,'tp'=4,'ep'=4] {'ep'}, dimensions={0} | all-to-all | bytes 2654208 | tf_op jit(solution)/shard_map/all_to_all | solution.py:53
  50.7 6.3 %fusion.9 = f32[4,1,54,2048]{3,2,0,1:T(8,128)S(1)} fusion(bf16[4,54,3072]{2,1,0:T(8,128)(2,1)S(1)} %all_to_all.21, bf16[1,3072,2048]{2,1,0:T(8,128)(2,1)} %param.9), kind=kOutput, calls=%fused_computation.8 | convolution fusion | flops 2717908992 | bytes 15679488 | tf_op jit(solution)/shard_map/tlcd,ldf->tlcf/dot_general | solution.py:33
  57.0 7.9 %fusion.18 = bf16[4,1,54,2048]{3,2,0,1:T(8,128)(2,1)S(1)} fusion(bf16[4,54,3072]{2,1,0:T(8,128)(2,1)S(1)} %all_to_all.21, bf16[1,3072,2048]{2,1,0:T(8,128)(2,1)} %param.10, f32[4,1,54,2048]{3,2,0,1:T(8,128)S(1)} %fusion.9), kind=kOutput, calls=%fused_computation.11 | convolution fusion | flops 2720563200 | bytes 16564224 | tf_op jit(solution)/shard_map/tlcd,ldf->tlcf/dot_general | solution.py:36
  64.9 0.2 dot_general.34
  65.1 9.0 %fusion.6 = f32[3072,216]{0,1:T(8,128)} fusion(bf16[216,2048]{1,0:T(8,128)(2,1)S(1)} %dot_general.34, bf16[1,2048,3072]{2,1,0:T(8,128)(2,1)} %param.11), kind=kOutput, calls=%fused_computation.6 | convolution fusion | flops 2717908992 | bytes 16121856 | tf_op jit(solution)/shard_map/tlcf,lfd->dtlc/dot_general | solution.py:57
  74.2 53.2 %reduce-scatter.2.cloned.1.call-done = f32[768,216]{0,1:T(8,128)} async-done(((f32[3072,216]{0,1:T(8,128)}), f32[768,216]{0,1:T(8,128)}) %reduce-scatter.2.cloned.1.call-update) | async-done | bytes 663568 | tf_op jit(solution)/shard_map/reduce_scatter | solution.py:58
  127.4 1.1 convert_bitcast_fusion
  128.5 0.1 all_to_all.16
  128.6 9.4 %all_to_all.22 = bf16[4,54,768]{2,1,0:T(8,128)(2,1)S(1)} all-to-all(bf16[4,54,768]{2,1,0:T(8,128)(2,1)S(1)} %all_to_all.16), channel_id=1, replica_groups=mesh['rep'=2,'tp'=4,'ep'=4] {'ep'}, dimensions={0} | all-to-all | bytes 663552 | tf_op jit(solution)/shard_map/all_to_all | solution.py:66
  138.0 0.1 all_to_all.18
  138.1 1.0 convolution_convert_fusion.1
  (10 shorter events, 0.2 us)
Async XLA Ops:
  6.5 120.8 %reduce-scatter.2.cloned.1.call-start = ((), (), s32[]{:S(2)}) async-start(), calls=%async_computation.3 | async-start | bytes 3317760 | tf_op jit(solution)/shard_map/reduce_scatter | solution.py:58
Sparse Core Ops, SparseCore 0:
  74.3 53.0 reduce-scatter.1
where the time goes:
time: 146 us
  waiting for transfers between devices  53.2 us (36%)
  blocking collectives  48.4 us (33%)
  matrix products  24.6 us (17%)
  between operations  13.5 us (9%)
  other arithmetic  4.01 us (3%)
  local copies, waits for them, and re-layouts  2.2 us (2%)
    reduce_scatter x1, waiting for transfers between devices, body(): lax.psum_scatter(part.reshape(columns // tp_count * lax.axis_size('tp'),...  53.2 us
    all_to_all x1, blocking collectives, body(): lax.all_to_all(packed, 'ep', split_axis=0, concat_axis=0, tiled=True)  20.5 us
    all_gather x1, blocking collectives, body(): whole = lax.all_gather(tokens, 'tp', axis=1, tiled=True)  18.5 us
    all_to_all x1, blocking collectives, body(): lax.all_to_all(expert_out, 'ep', split_axis=0, concat_axis=0, tiled=True)  9.41 us
    dot_general x1, matrix products, body(): jnp.einsum('tlcf,lfd->dtlc', hidden, expert_down, preferred_element_type=...  9.01 us
    dot_general x1, matrix products, hidden_rows(): jnp.einsum('tlcd,ldf->tlcf', row_block, expert_up, preferred_element_type...  7.89 us
    dot_general x1, matrix products, hidden_rows(): jnp.einsum('tlcd,ldf->tlcf', row_block, expert_gate, preferred_element_ty...  6.26 us
  transfers between devices with their start and end apart: 1, of which 1 were waited for; matrix products, arithmetic and copies ran while one was open for 0% of the time, Pallas kernels for 0%

commit v1 on v0

--- a/solution.py
+++ b/solution.py
@@ -2,6 +2,26 @@
 import jax.numpy as jnp
 from jax import lax
 from jax.sharding import PartitionSpec as P
+from jax.lax import axis_index, axis_size, ppermute
+
+
+def remake_types(local_values, shard_axis, local_block):
+    v_next = axis_size(shard_axis)
+    row_list = []
+    i0 = 0
+    later, arr_out, known = (v_next, axis_index(shard_axis), local_values.shape[1])
+    while i0 < later:
+        k_now = (
+            ppermute(local_values, shard_axis, [(no, (no + 1) % later) for no in range(later)])
+            if i0 + 1 < later
+            else local_values
+        )
+        row_list.append(local_block(local_values, (arr_out - i0) % later * known))
+        local_values = k_now
+        i0 += 1
+    opened = jnp.concatenate(row_list[::-1], axis=1)
+    current_block = jnp.roll(opened, (arr_out + 1) * row_list[0].shape[1], axis=1)
+    return current_block
 
 
 def slot_tables(routing, route_gates, experts, capacity):
@@ -46,9 +66,12 @@
     experts = local_count * ep_count
     dispatch, combine = slot_tables(routing, route_gates, experts, capacity)
     dispatch_low = dispatch.astype(jnp.bfloat16)
-    whole = lax.all_gather(tokens, "tp", axis=1, tiled=True)
-    packed = jnp.einsum(
-        "tc,td->cd", dispatch_low, whole, preferred_element_type=jnp.float32
+    packed = remake_types(
+        tokens,
+        "tp",
+        lambda part_2, start: jnp.einsum(
+            "tc,td->cd", dispatch_low, part_2, preferred_element_type=jnp.float32
+        ),
     ).astype(jnp.bfloat16)
     everyone = lax.all_to_all(packed, "ep", split_axis=0, concat_axis=0, tiled=True)
     total_rows = everyone.shape[0]

time: 146 us -> 145 us (level)
  blocking collectives: 48.4 us -> 29.9 us
  waiting for transfers between devices: 53.2 us -> 66 us
  starting transfers between devices: 0.01 us -> 3.06 us
    all_gather x1 -> x0, blocking collectives: 18.5 us -> none  [body(): whole = lax.all_gather(tokens, 'tp', axis=1, tiled=True)]
    ppermute x0 -> x3, waiting for transfers between devices: none -> 15.7 us  [remake_types(): ppermute(local_values, shard_axis, [(no, (no + 1) % later) for no in rang...]
    ppermute x0 -> x3, starting transfers between devices: none -> 3.06 us  [remake_types(): ppermute(local_values, shard_axis, [(no, (no + 1) % later) for no in rang...]
    reduce_scatter x1, waiting for transfers between devices: 53.2 us -> 50.2 us  [body(): lax.psum_scatter(part.reshape(columns // tp_count * lax.axis_size('tp'),...]
  transfers between devices with their start and end apart: 1 -> 4, of which waited for: 1 -> 4; matrix products, arithmetic and copies ran while one was open for 0% -> 3% of each run, Pallas kernels for 0% -> 0%
where the time goes in v1:
time: 145 us; the launch traced here: 144 us
  waiting for transfers between devices  66 us (46%)
  blocking collectives  29.9 us (21%)
  matrix products  25.2 us (17%)
  between operations  13.5 us (9%)
  other arithmetic  3.98 us (3%)
  starting transfers between devices  3.06 us (2%)
  local copies, waits for them, and re-layouts  2.84 us (2%)
    reduce_scatter x1, waiting for transfers between devices, body(): lax.psum_scatter(part.reshape(columns // tp_count * lax.axis_size('tp'),...  50.2 us
    all_to_all x1, blocking collectives, body(): lax.all_to_all(packed, 'ep', split_axis=0, concat_axis=0, tiled=True)  20.5 us
    ppermute x3, waiting for transfers between devices, remake_types(): ppermute(local_values, shard_axis, [(no, (no + 1) % later) for no in rang...  15.7 us
    all_to_all x1, blocking collectives, body(): lax.all_to_all(expert_out, 'ep', split_axis=0, concat_axis=0, tiled=True)  9.41 us
    dot_general x1, matrix products, body(): jnp.einsum('tlcf,lfd->dtlc', hidden, expert_down, preferred_element_type=...  9.01 us
    dot_general x1, matrix products, hidden_rows(): jnp.einsum('tlcd,ldf->tlcf', row_block, expert_up, preferred_element_type...  7.89 us
    dot_general x1, matrix products, hidden_rows(): jnp.einsum('tlcd,ldf->tlcf', row_block, expert_gate, preferred_element_ty...  6.25 us
    ppermute x3, starting transfers between devices, remake_types(): ppermute(local_values, shard_axis, [(no, (no + 1) % later) for no in rang...  3.06 us
  transfers between devices with their start and end apart: 4, of which 4 were waited for; matrix products, arithmetic and copies ran while one was open for 3% of the time, Pallas kernels for 0%

profile of v1, /device:TPU:0, one launch (start us, length us, event | category | flops | bytes accessed | tf_op | source)
XLA Modules:
  0.0 144.5 jit_solution(7979003311763664559)
XLA Ops:
  6.5 3.1 %collective-permute-start = (bf16[96,768]{1,0:T(8,128)(2,1)}, bf16[96,768]{1,0:T(8,128)(2,1)S(1)}, u32[]{:S(2)}, u32[]{:S(2)}) collective-permute-start(bf16[96,768]{1,0:T(8,128)(2,1)} %param.6), channel_id=1, source_target_pairs={{0,4},{4,8},{8,12},{12,0},{1,5},{5,9},{9,13},{13,1},{2,6},{6,10},{... | collective-permute-start | bytes 442376 | tf_op jit(solution)/shard_map/ppermute | solution.py:15
  9.6 0.8 copy.23
  10.5 1.2 reduce-window.6
  12.1 3.7 %collective-permute-done = bf16[96,768]{1,0:T(8,128)(2,1)S(1)} collective-permute-done((bf16[96,768]{1,0:T(8,128)(2,1)}, bf16[96,768]{1,0:T(8,128)(2,1)S(1)}, u32[]{:S(2)}, u32[]{:S(2)}) %collective-permute-start) | collective-permute-done | bytes 147488 | tf_op jit(solution)/shard_map/ppermute | solution.py:15
  15.8 0.1 reduce_sum.30
  16.1 6.6 %collective-permute-done.1 = bf16[96,768]{1,0:T(8,128)(2,1)S(1)} collective-permute-done((bf16[96,768]{1,0:T(8,128)(2,1)S(1)}, bf16[96,768]{1,0:T(8,128)(2,1)S(1)}, u32[]{:S(2)}, u32[]{:S(2)}) %collective-permute-start.1) | collective-permute-done | bytes 147488 | tf_op jit(solution)/shard_map/ppermute | solution.py:15
  22.7 0.7 multiply_add_fusion
  23.4 0.8 convert_reduce_fusion
  24.2 5.4 %collective-permute-done.2 = bf16[96,768]{1,0:T(8,128)(2,1)S(1)} collective-permute-done((bf16[96,768]{1,0:T(8,128)(2,1)S(1)}, bf16[96,768]{1,0:T(8,128)(2,1)S(1)}, u32[]{:S(2)}, u32[]{:S(2)}) %collective-permute-start.2) | collective-permute-done | bytes 147488 | tf_op jit(solution)/shard_map/ppermute | solution.py:15
  29.6 0.3 constant_dynamic-update-slice_fusion.7
  29.9 0.3 constant_dynamic-update-slice_fusion.6
  30.2 0.3 constant_dynamic-update-slice_fusion.5
  30.5 0.3 constant_dynamic-update-slice_fusion.4
  30.9 0.5 dynamic-slice_convert_fusion
  31.4 0.4 all_to_all.14
  31.8 20.5 %all_to_all.21 = bf16[4,54,3072]{2,1,0:T(8,128)(2,1)S(1)} all-to-all(bf16[4,54,3072]{2,1,0:T(8,128)(2,1)S(1)} %all_to_all.14), channel_id=1, replica_groups=mesh['rep'=2,'tp'=4,'ep'=4] {'ep'}, dimensions={0} | all-to-all | bytes 2654208 | tf_op jit(solution)/shard_map/all_to_all | solution.py:76
  52.3 6.3 %fusion.9 = f32[4,1,54,2048]{3,2,0,1:T(8,128)S(1)} fusion(bf16[4,54,3072]{2,1,0:T(8,128)(2,1)S(1)} %all_to_all.21, bf16[1,3072,2048]{2,1,0:T(8,128)(2,1)} %param.9), kind=kOutput, calls=%fused_computation.7 | convolution fusion | flops 2717908992 | bytes 15679488 | tf_op jit(solution)/shard_map/tlcd,ldf->tlcf/dot_general | solution.py:53
  58.6 7.9 %fusion.18 = bf16[4,1,54,2048]{3,2,0,1:T(8,128)(2,1)S(1)} fusion(bf16[4,54,3072]{2,1,0:T(8,128)(2,1)S(1)} %all_to_all.21, bf16[1,3072,2048]{2,1,0:T(8,128)(2,1)} %param.10, f32[4,1,54,2048]{3,2,0,1:T(8,128)S(1)} %fusion.9), kind=kOutput, calls=%fused_computation.11 | convolution fusion | flops 2720563200 | bytes 16564224 | tf_op jit(solution)/shard_map/tlcd,ldf->tlcf/dot_general | solution.py:56
  66.5 0.2 dot_general.46
  66.7 9.0 %fusion.6 = f32[3072,216]{0,1:T(8,128)} fusion(bf16[216,2048]{1,0:T(8,128)(2,1)S(1)} %dot_general.46, bf16[1,2048,3072]{2,1,0:T(8,128)(2,1)} %param.11), kind=kOutput, calls=%fused_computation.6 | convolution fusion | flops 2717908992 | bytes 16121856 | tf_op jit(solution)/shard_map/tlcf,lfd->dtlc/dot_general | solution.py:80
  75.7 50.2 %reduce-scatter.2.cloned.1.call-done = f32[768,216]{0,1:T(8,128)} async-done(((f32[3072,216]{0,1:T(8,128)}), f32[768,216]{0,1:T(8,128)}) %reduce-scatter.2.cloned.1.call-update) | async-done | bytes 663568 | tf_op jit(solution)/shard_map/reduce_scatter | solution.py:81
  126.0 1.1 convert_bitcast_fusion
  127.2 9.4 %all_to_all.22 = bf16[4,54,768]{2,1,0:T(8,128)(2,1)S(1)} all-to-all(bf16[4,54,768]{2,1,0:T(8,128)(2,1)S(1)} %all_to_all.16), channel_id=1, replica_groups=mesh['rep'=2,'tp'=4,'ep'=4] {'ep'}, dimensions={0} | all-to-all | bytes 663552 | tf_op jit(solution)/shard_map/all_to_all | solution.py:89
  136.7 1.0 convolution_convert_fusion
  (25 shorter events, 1.0 us)
Async XLA Ops:
  6.5 23.9 %copy-start = (bf16[96,768]{1,0:T(8,128)(2,1)S(1)}, bf16[96,768]{1,0:T(8,128)(2,1)}, u32[]{:S(2)}) copy-start(bf16[96,768]{1,0:T(8,128)(2,1)} %param.6) | copy-start | bytes 442372
  6.5 119.4 %reduce-scatter.2.cloned.1.call-start = ((), (), s32[]{:S(2)}) async-start(), calls=%async_computation.3 | async-start | bytes 3317760 | tf_op jit(solution)/shard_map/reduce_scatter | solution.py:81
  6.5 9.2 %collective-permute-start = (bf16[96,768]{1,0:T(8,128)(2,1)}, bf16[96,768]{1,0:T(8,128)(2,1)S(1)}, u32[]{:S(2)}, u32[]{:S(2)}) collective-permute-start(bf16[96,768]{1,0:T(8,128)(2,1)} %param.6), channel_id=1, source_target_pairs={{0,4},{4,8},{8,12},{12,0},{1,5},{5,9},{9,13},{13,1},{2,6},{6,10},{... | collective-permute-start | bytes 442376 | tf_op jit(solution)/shard_map/ppermute | solution.py:15
  15.7 6.9 %collective-permute-start.1 = (bf16[96,768]{1,0:T(8,128)(2,1)S(1)}, bf16[96,768]{1,0:T(8,128)(2,1)S(1)}, u32[]{:S(2)}, u32[]{:S(2)}) collective-permute-start(bf16[96,768]{1,0:T(8,128)(2,1)S(1)} %collective-permute-done), channel_id=1, source_target_pairs={{0,4},{4,8},{8,12},{12,0},{1,5},{5,9},{9,13},{13,1},{2,6},{6,10},{... | collective-permute-start | bytes 442376 | tf_op jit(solution)/shard_map/ppermute | solution.py:15
  22.7 6.9 %collective-permute-start.2 = (bf16[96,768]{1,0:T(8,128)(2,1)S(1)}, bf16[96,768]{1,0:T(8,128)(2,1)S(1)}, u32[]{:S(2)}, u32[]{:S(2)}) collective-permute-start(bf16[96,768]{1,0:T(8,128)(2,1)S(1)} %collective-permute-done.1), channel_id=1, source_target_pairs={{0,4},{4,8},{8,12},{12,0},{1,5},{5,9},{9,13},{13,1},{2,6},{6,10},{... | collective-permute-start | bytes 442376 | tf_op jit(solution)/shard_map/ppermute | solution.py:15
Sparse Core Ops, SparseCore 0:
  75.9 50.0 reduce-scatter.1
